TPU v7x, 256 devices: a whole 4x4x8 slice. The times are simulated.
256 devices in a mesh: section: 16 (over y, z_hi, core), dp: 16 (over x, z_lo).
Axes of the slice: x: 4, y: 4, z: 8 (z_hi: 2, z_lo: 4; z = z_hi * 4 + z_lo), core: 2. Of those that a mesh axis runs over, the one named last changes fastest.
Arguments:
- student_states: bfloat16 [16, 2048, 2048], P('section', 'dp'), may hold values from -6 to 6
- teacher_states: bfloat16 [64, 2048, 7168], P('section', 'dp'), may hold values from -18 to 18
- projector: bfloat16 [16, 2048, 7168], P('section', None, 'dp'), may hold values from -0.125 to 0.125
- layer_map: int32 [16], replicated, may hold values from 0 to 60, as said below
- boundaries: int32 [17], replicated, may hold values from 0 to 61, as said below
- valid_counts: int32 [16], P('dp'), may hold values from 32 to 128, as said below
Outputs:
- student_grads: bfloat16 [16, 2048, 2048], P('section', 'dp')
- projector_grads: bfloat16 [16, 2048, 7168], P('section', None, 'dp')
- layer_losses: float32 [16], P('section')
Inputs may be any that keep to these rules, and one draw needn't show every extreme that they name: Section k holds 4 or 3 teacher layers, three sections the smaller number; boundaries[0] is 0 and boundaries[16] is 61. Teacher layer layer_map[l] lies on a section from l - 2 to l + 2; student layers 0 and 15 pair with layers of sections 1 and 14, student layers 1 and 14 with layers of sections 3 and 12. `valid_counts`: the valid tokens stand first in their micro-batch; the last micro-batch is full.
All inputs are finite; a program needn't handle non-finite values.
Results may differ from a plain program's by a relative error of at most 0.015.
Values may be sent and summed in bfloat16 or wider, within the bound.
No kernel may reach another device: no remote copies, remote signals or barrier semaphores. Data moves between devices by JAX's collectives and lax.ppermute only.
A program may use at most 128 MiB of HBM per device.

v0:
```python
import jax
import jax.numpy as jnp
from jax import lax
from jax.sharding import Mesh
from jax.sharding import PartitionSpec as P

DP = ("dp_0", "dp_1")
loss_scale = 128.0
norm_eps = 1e-06


def from_behind(block, axis, distance):
    devices = range(lax.axis_size(axis))
    route = [(i - distance, i) for i in devices if i - distance in devices]
    return lax.ppermute(block, axis, route)


def whole_of(x, axes, dim):
    for axis in reversed(axes):
        x = lax.all_gather(x, axis, axis=dim, tiled=True)
    return x


def copy_for_each(x, axis):
    copies = jnp.broadcast_to(x, (lax.axis_size(axis), *x.shape))
    return lax.all_to_all(copies, axis, split_axis=0, concat_axis=0, tiled=True)


def over_copies(x, axis):
    everything = copy_for_each(x, axis)
    return jnp.sum(everything, axis=0)


def lookup(table, index):
    places = jnp.arange(table.shape[0], dtype=jnp.int32)
    return jnp.sum(jnp.where(places == index, table, 0))


def direct_step(piece, offset):
    return from_behind(piece, "section", offset)


def per_device(student_states, teacher_states, projector, layer_map, boundaries, valid_counts):
    sections = lax.axis_size("section")
    here = lax.axis_index("section")
    held_slots = teacher_states.shape[0]
    inner = boundaries[1:sections]
    owners = jnp.sum((inner[None, :] <= layer_map[:, None]).astype(jnp.int32), axis=1)
    first_layer = lookup(boundaries, here)

    def outgoing(offset):
        destination = here + offset
        inside = (destination >= 0) & (destination < sections)
        wanted = lookup(layer_map, destination)
        owner = lookup(owners, destination)
        place = jnp.clip(wanted - first_layer, 0, held_slots - 1)
        piece = lax.dynamic_index_in_dim(teacher_states, place, 0, keepdims=False)
        return jnp.where(inside & (owner == here), piece, jnp.zeros_like(piece))

    needed = here - lookup(owners, here)
    arrivals = []
    for offset in (-2, -1, 1, 2):
        arrivals.append((offset, direct_step(outgoing(offset), offset)))
    hidden = outgoing(0)
    for offset, arrived in arrivals:
        hidden = jnp.where(needed == offset, arrived, hidden)
    wide = hidden.astype(jnp.float32)
    target = (wide * lax.rsqrt(jnp.mean(wide * wide, axis=1, keepdims=True) + norm_eps)).astype(
        jnp.bfloat16
    )
    columns = lax.all_to_all(target, DP, split_axis=1, concat_axis=0, tiled=True)
    students, counts = (whole_of(student_states[0], DP, 0), whole_of(valid_counts, DP, 0))
    per_batch = student_states.shape[1]
    token_rows = jnp.arange(students.shape[0], dtype=jnp.int32)
    batch_index = token_rows // per_batch
    batches = jnp.arange(counts.shape[0], dtype=jnp.int32)
    limit = jnp.sum(jnp.where(batch_index[:, None] == batches[None, :], counts[None, :], 0), axis=1)
    valid = (token_rows % per_batch < limit).astype(jnp.float32)[:, None]
    total = jnp.sum(counts).astype(jnp.float32)
    weights = projector[0]
    projected = jnp.dot(students, weights, preferred_element_type=jnp.float32)
    residual = projected - columns.astype(jnp.float32)
    squares = jnp.sum(valid * residual * residual)
    teacher_width = weights.shape[1] * lax.axis_size(DP)
    loss = over_copies(squares, DP) / (total * teacher_width)
    scaled = (valid * (loss_scale / total) * residual).astype(jnp.bfloat16)
    student_grad = lax.psum_scatter(
        lax.dot_general(
            scaled, weights, (((1,), (1,)), ((), ())), preferred_element_type=jnp.float32
        ).astype(jnp.bfloat16),
        DP,
        scatter_dimension=0,
        tiled=True,
    )
    projector_grad = lax.dot_general(
        students, scaled, (((0,), (0,)), ((), ())), preferred_element_type=jnp.float32
    ).astype(jnp.bfloat16)
    return (student_grad[None], projector_grad[None], jnp.reshape(loss, (1,)))


def solution(mesh):
    split = Mesh(mesh.devices.reshape(mesh.shape["section"], 4, 4), ("section", "dp_0", "dp_1"))
    return jax.shard_map(
        per_device,
        mesh=split,
        in_specs=(
            P("section", DP, None),
            P("section", DP, None),
            P("section", None, DP),
            P(),
            P(),
            P(DP),
        ),
        out_specs=(P("section", DP, None), P("section", None, DP), P("section")),
        check_vma=False,
    )
```

profile of v0, /device:TPU:1, one launch (start us, length us, event | category | flops | bytes accessed | tf_op | source)
XLA Modules:
  0.0 574.9 jit_solution(18182196803726800490)
XLA Ops:
  7.2 0.0 copy-start
  7.2 0.0 all-gather.5.cloned.1.call-start
  7.2 0.7 all-gather.5.cloned.1.call-update
  7.9 0.0 all-gather.7.cloned.1.call-start
  8.0 0.7 slice.3
  8.7 1.4 fusion.36
  10.1 0.8 convert_reduce_fusion
  10.9 1.5 fusion.26
  19.4 7.4 %constant_dynamic-slice_fusion = (bf16[1,128,7168]{2,1,0:T(8,128)(2,1)}, bf16[1,128,7168]{2,1,0:T(8,128)(2,1)}, bf16[1,128,7168]{2,1,0:T(8,128)(2,1)}, bf16[1,128,7168]{2,1,0:T(8,128)(2,1)}, bf16[1,128,7168]{2,1,0:T(8,128)(2,1)}) fusion(bf16[4,128,7168]{2,1,0:T(8,128)(2,1)} %param.7, s32[]{:T(128)S(6)} %min.20, s32[]{:T(128)S(6)} %min.19, s32[]{:T(128)S(6)} %min.18, ...), kind=kLoop, calls=%fused_computation.42 | loop fusion | bytes 18350100 | tf_op jit(solution)/shard_map/jit(dynamic_index_in_dim)/dynamic_slice | solution.py:57
  26.8 3.9 copy.30
  30.7 2.9 select_bitcast_fusion.3
  33.6 9.7 %collective-permute-start = (bf16[128,7168]{0,1:T(8,128)(2,1)}, bf16[128,7168]{0,1:T(8,128)(2,1)}, u32[]{:S(2)}, u32[]{:S(2)}) collective-permute-start(bf16[128,7168]{0,1:T(8,128)(2,1)} %select_bitcast_fusion.3), channel_id=1, source_target_pairs={{0,32},{16,48},{32,64},{48,80},{64,96},{80,112},{96,128},{112,144}... | collective-permute-start | bytes 5505032 | tf_op jit(solution)/shard_map/ppermute | solution.py:15
  44.0 3.9 copy.31
  47.9 41.0 %all-gather.5.cloned.1.call-done = bf16[1,512,2048]{2,1,0:T(8,128)(2,1)} async-done(((bf16[1,128,2048]{2,1,0:T(8,128)(2,1)}), bf16[1,512,2048]{2,1,0:T(8,128)(2,1)}) %all-gather.5.cloned.1.call-update) | async-done | bytes 2097168 | tf_op jit(solution)/shard_map/all_gather | solution.py:20
  88.9 0.0 all-gather.7.cloned.1.call-update
  89.0 1.4 select_bitcast_fusion.2
  90.3 12.4 %collective-permute-start.1 = (bf16[128,7168]{0,1:T(8,128)(2,1)}, bf16[128,7168]{0,1:T(8,128)(2,1)}, u32[]{:S(2)}, u32[]{:S(2)}) collective-permute-start(bf16[128,7168]{0,1:T(8,128)(2,1)} %select_bitcast_fusion.2), channel_id=1, source_target_pairs={{0,16},{16,32},{32,48},{48,64},{64,80},{80,96},{96,112},{112,128},... | collective-permute-start | bytes 5505032 | tf_op jit(solution)/shard_map/ppermute | solution.py:15
  103.3 3.9 copy.32
  107.2 2.9 select_bitcast_fusion.1
  110.1 1.9 collective-permute-start.2
  112.7 3.9 copy.33
  116.5 1.4 select_bitcast_fusion
  118.0 1.3 collective-permute-start.3
  120.6 3.9 copy.34
  124.5 0.0 collective-permute-done
  124.5 17.2 %collective-permute-done.1 = bf16[128,7168]{0,1:T(8,128)(2,1)} collective-permute-done((bf16[128,7168]{0,1:T(8,128)(2,1)}, bf16[128,7168]{0,1:T(8,128)(2,1)}, u32[]{:S(2)}, u32[]{:S(2)}) %collective-permute-start.1) | collective-permute-done | bytes 1835040 | tf_op jit(solution)/shard_map/ppermute | solution.py:15
  141.6 63.3 %collective-permute-done.2 = bf16[128,7168]{0,1:T(8,128)(2,1)} collective-permute-done((bf16[128,7168]{0,1:T(8,128)(2,1)}, bf16[128,7168]{0,1:T(8,128)(2,1)}, u32[]{:S(2)}, u32[]{:S(2)}) %collective-permute-start.2) | collective-permute-done | bytes 1835040 | tf_op jit(solution)/shard_map/ppermute | solution.py:15
  204.9 38.3 %collective-permute-done.3 = bf16[128,7168]{0,1:T(8,128)(2,1)} collective-permute-done((bf16[128,7168]{0,1:T(8,128)(2,1)}, bf16[128,7168]{0,1:T(8,128)(2,1)}, u32[]{:S(2)}, u32[]{:S(2)}) %collective-permute-start.3) | collective-permute-done | bytes 1835040 | tf_op jit(solution)/shard_map/ppermute | solution.py:15
  243.2 3.3 fusion.4
  246.5 1.6 fusion.5
  248.1 0.0 copy-start.3
  248.1 0.0 copy-start.2
  248.1 63.7 %all-to-all-start = ((bf16[128,16,448]{0,2,1:T(8,128)(2,1)}), bf16[128,16,448]{0,2,1:T(8,128)(2,1)}, u32[]{:S(2)}, u32[]{:S(2)}) async-start(bf16[128,16,448]{0,2,1:T(8,128)(2,1)} %bitcast.52), calls=%async_computation | async-start | bytes 3670016 | tf_op jit(solution)/shard_map/all_to_all | solution.py:71
  311.8 0.0 reduce-scatter.2.cloned.1.call-start
  312.5 0.0 copy-done.3
  312.5 0.6 dynamic-slice
  313.1 0.8 dynamic-update-slice
  313.8 39.9 %all-reduce = s32[4]{0:T(128)S(1)} all-reduce(s32[4]{0:T(128)S(1)} %dynamic-update-slice), channel_id=1, replica_groups=mesh['section'=16,'dp_0'=4,'dp_1'=4] {'dp_1'}, use_global_device_ids=true, to_apply=%add | all-reduce | flops 4 | bytes 32
  353.7 0.0 copy-done.2
  353.7 0.6 dynamic-slice.1
  354.9 0.2 dynamic-update-slice.1
  355.2 7.2 %all-reduce.1 = s32[16]{0:T(128)S(1)} all-reduce(s32[16]{0:T(128)S(1)} %dynamic-update-slice.1), channel_id=1, replica_groups=mesh['section'=16,'dp_0'=4,'dp_1'=4] {'dp_0'}, use_global_device_ids=true, to_apply=%add.1 | all-reduce | flops 16 | bytes 128
  362.4 0.6 reduce_sum.158
  363.7 0.1 select_reduce_fusion
  363.9 0.0 all-to-all-done
  363.9 0.0 all-gather.7.cloned.1.call-done
  363.9 0.0 copy-done
  363.9 8.6 %fusion.6 = (f32[]{:T(128)}, f32[2048,448]{0,1:T(8,128)S(1)}) fusion(f32[2048]{0:T(1024)S(1)} %get-tuple-element.13, bf16[1,2048,448]{1,2,0:T(8,128)(2,1)S(1)} %copy-done, bf16[1,2048,2048]{2,1,0:T(8,128)(2,1)} %all-gather.7.cloned.1.call-done, bf16[128,16,448]{0,2,1:T(8,128)(2,1)} %all-to-all-done), kind=kOutput, calls=%fused_computation.10 | convolution fusion | flops 3762683904 | bytes 15736836 | tf_op jit(solution)/shard_map/dot_general | solution.py:81
  372.5 0.0 copy-start.4
  372.5 1.8 copy-done.4
  374.3 6.8 %convolution_convert_fusion = bf16[2048,2048]{1,0:T(8,128)(2,1)} fusion(bf16[1,2048,448]{1,2,0:T(8,128)(2,1)S(1)} %copy-done, f32[2048,448]{0,1:T(8,128)S(1)} %get-tuple-element.23, f32[2048]{0:T(1024)S(1)} %broadcast_select_fusion), kind=kOutput, calls=%fused_computation.4 | convolution fusion | flops 3764125696 | bytes 13901824 | tf_op jit(solution)/shard_map/dot_general | solution.py:88
  381.1 0.0 reduce-scatter.2.cloned.1.call-update
  381.2 1.2 broadcast_in_dim.52
  382.4 4.3 all-to-all-start.1
  386.7 0.0 copy-start.1
  386.7 9.8 %fusion.12 = bf16[1,2048,448]{1,2,0:T(8,128)(2,1)} fusion(bf16[1,2048,2048]{2,1,0:T(8,128)(2,1)} %all-gather.7.cloned.1.call-done, f32[2048,448]{0,1:T(8,128)} %copy-done.4, f32[2048]{0:T(1024)S(1)} %broadcast_select_fusion), kind=kOutput, calls=%fused_computation.15 | convolution fusion | flops 3760848896 | bytes 13901824 | tf_op jit(solution)/shard_map/dot_general | solution.py:95
  396.5 0.0 all-to-all-done.1
  396.5 0.6 reduce_sum.173
  397.8 169.4 %reduce-scatter.2.cloned.1.call-done = bf16[128,2048]{1,0:T(8,128)(2,1)} async-done(((bf16[2048,2048]{1,0:T(8,128)(2,1)}), bf16[128,2048]{1,0:T(8,128)(2,1)}) %reduce-scatter.2.cloned.1.call-update) | async-done | bytes 524304 | tf_op jit(solution)/shard_map/reduce_scatter | solution.py:87
  567.2 0.0 copy-done.1
  (6 shorter events, 0.0 us)
Async XLA Ops:
  7.2 356.7 %copy-start = (bf16[1,2048,448]{1,2,0:T(8,128)(2,1)S(1)}, bf16[1,2048,448]{1,2,0:T(8,128)(2,1)}, u32[]{:S(2)}) copy-start(bf16[1,2048,448]{1,2,0:T(8,128)(2,1)} %param.8) | copy-start | bytes 5505028
  7.2 81.7 %all-gather.5.cloned.1.call-start = ((), (), s32[]{:S(2)}) async-start(), calls=%async_computation.4 | async-start | bytes 2621440 | tf_op jit(solution)/shard_map/all_gather | solution.py:20
  7.9 356.0 %all-gather.7.cloned.1.call-start = ((), (), s32[]{:S(2)}) async-start(), calls=%async_computation.5 | async-start | bytes 10485760 | tf_op jit(solution)/shard_map/all_gather | solution.py:20
  33.6 90.9 %collective-permute-start = (bf16[128,7168]{0,1:T(8,128)(2,1)}, bf16[128,7168]{0,1:T(8,128)(2,1)}, u32[]{:S(2)}, u32[]{:S(2)}) collective-permute-start(bf16[128,7168]{0,1:T(8,128)(2,1)} %select_bitcast_fusion.3), channel_id=1, source_target_pairs={{0,32},{16,48},{32,64},{48,80},{64,96},{80,112},{96,128},{112,144}... | collective-permute-start | bytes 5505032 | tf_op jit(solution)/shard_map/ppermute | solution.py:15
  90.3 51.3 %collective-permute-start.1 = (bf16[128,7168]{0,1:T(8,128)(2,1)}, bf16[128,7168]{0,1:T(8,128)(2,1)}, u32[]{:S(2)}, u32[]{:S(2)}) collective-permute-start(bf16[128,7168]{0,1:T(8,128)(2,1)} %select_bitcast_fusion.2), channel_id=1, source_target_pairs={{0,16},{16,32},{32,48},{48,64},{64,80},{80,96},{96,112},{112,128},... | collective-permute-start | bytes 5505032 | tf_op jit(solution)/shard_map/ppermute | solution.py:15
  110.1 94.8 %collective-permute-start.2 = (bf16[128,7168]{0,1:T(8,128)(2,1)}, bf16[128,7168]{0,1:T(8,128)(2,1)}, u32[]{:S(2)}, u32[]{:S(2)}) collective-permute-start(bf16[128,7168]{0,1:T(8,128)(2,1)} %select_bitcast_fusion.1), channel_id=1, source_target_pairs={{16,0},{32,16},{48,32},{64,48},{80,64},{96,80},{112,96},{128,112},... | collective-permute-start | bytes 5505032 | tf_op jit(solution)/shard_map/ppermute | solution.py:15
  118.0 125.2 %collective-permute-start.3 = (bf16[128,7168]{0,1:T(8,128)(2,1)}, bf16[128,7168]{0,1:T(8,128)(2,1)}, u32[]{:S(2)}, u32[]{:S(2)}) collective-permute-start(bf16[128,7168]{0,1:T(8,128)(2,1)} %select_bitcast_fusion), channel_id=1, source_target_pairs={{32,0},{48,16},{64,32},{80,48},{96,64},{112,80},{128,96},{144,112}... | collective-permute-start | bytes 5505032 | tf_op jit(solution)/shard_map/ppermute | solution.py:15
  248.1 64.4 %copy-start.3 = (u32[256]{0:T(256)S(1)}, u32[256]{0:T(256)}, u32[]{:S(2)}) copy-start(u32[256]{0:T(256)} %constant.84) | copy-start | bytes 3076
  248.1 105.6 %copy-start.2 = (u32[256]{0:T(256)S(1)}, u32[256]{0:T(256)}, u32[]{:S(2)}) copy-start(u32[256]{0:T(256)} %constant.89) | copy-start | bytes 3076
  248.1 115.8 %all-to-all-start = ((bf16[128,16,448]{0,2,1:T(8,128)(2,1)}), bf16[128,16,448]{0,2,1:T(8,128)(2,1)}, u32[]{:S(2)}, u32[]{:S(2)}) async-start(bf16[128,16,448]{0,2,1:T(8,128)(2,1)} %bitcast.52), calls=%async_computation | async-start | bytes 3670016 | tf_op jit(solution)/shard_map/all_to_all | solution.py:71
  311.8 255.5 %reduce-scatter.2.cloned.1.call-start = ((), (), s32[]{:S(2)}) async-start(), calls=%async_computation.3 | async-start | bytes 8912896 | tf_op jit(solution)/shard_map/reduce_scatter | solution.py:87
  372.5 1.8 copy-start.4
  382.4 14.1 %all-to-all-start.1 = ((f32[16,1,1]{2,1,0:T(1,128)}), f32[16,1,1]{2,1,0:T(1,128)S(1)}, u32[]{:S(2)}, u32[]{:S(2)}) async-start(f32[16,1,1]{2,1,0:T(1,128)} %broadcast_in_dim.52), calls=%async_computation.2 | async-start | bytes 16384 | tf_op jit(solution)/shard_map/all_to_all | solution.py:26
  386.7 180.5 %copy-start.1 = (bf16[1,2048,448]{1,2,0:T(8,128)(2,1)S(1)}, bf16[1,2048,448]{1,2,0:T(8,128)(2,1)}, u32[]{:S(2)}) copy-start(bf16[1,2048,448]{1,2,0:T(8,128)(2,1)} %param.8) | copy-start | bytes 5505028
Sparse Core Ops, SparseCore 0:
  9.8 79.0 all-gather.4
  90.7 227.4 all-gather.6
  381.3 185.9 reduce-scatter.1
where the time goes:
time: 576 us; the launch traced here: 575 us
  waiting for transfers between devices  330 us (57%)
  starting transfers between devices  93.4 us (16%)
  blocking collectives  47.1 us (8%)
  local copies, waits for them, and re-layouts  32.8 us (6%)
  between operations  27.9 us (5%)
  matrix products  25.2 us (4%)
  other arithmetic  18.5 us (3%)
    reduce_scatter x1, waiting for transfers between devices, per_device(): lax.psum_scatter(lax.dot_general(scaled, weights, (((1,), (1,)), ((), ())...  169 us
    ppermute x4, waiting for transfers between devices, from_behind(): return lax.ppermute(block, axis, route)  119 us
    all_to_all x1, starting transfers between devices, per_device(): lax.all_to_all(target, DP, split_axis=1, concat_axis=0, tiled=True)  63.7 us
    unnamed x2, blocking collectives  47.1 us
    all_gather x2, waiting for transfers between devices, whole_of(): x = lax.all_gather(x, axis, axis=dim, tiled=True)  41 us
    ppermute x4, starting transfers between devices, from_behind(): return lax.ppermute(block, axis, route)  25.3 us
    unnamed x21, local copies, waits for them, and re-layouts  23.5 us
  transfers between devices with their start and end apart: 9, of which 5 were waited for; matrix products, arithmetic and copies ran while one was open for 10% of the time, Pallas kernels for 0%

commit v1 on v0

--- a/solution.py
+++ b/solution.py
@@ -68,7 +68,9 @@
     target = (wide * lax.rsqrt(jnp.mean(wide * wide, axis=1, keepdims=True) + norm_eps)).astype(
         jnp.bfloat16
     )
-    columns = lax.all_to_all(target, DP, split_axis=1, concat_axis=0, tiled=True)
+    columns = jnp.concatenate(
+        lax.all_to_all(jnp.stack(jnp.split(target, lax.axis_size(DP), axis=1)), DP, 0, 0), axis=0
+    )
     students, counts = (whole_of(student_states[0], DP, 0), whole_of(valid_counts, DP, 0))
     per_batch = student_states.shape[1]
     token_rows = jnp.arange(students.shape[0], dtype=jnp.int32)

time: 576 us -> 586 us (1.017)
  local copies, waits for them, and re-layouts: 32.8 us -> 43.4 us
  waiting for transfers between devices: 330 us -> 340 us
  starting transfers between devices: 93.4 us -> 84.3 us
    ppermute x4, waiting for transfers between devices: 119 us -> 146 us  [from_behind(): return lax.ppermute(block, axis, route)]
    all_gather x2, waiting for transfers between devices: 41 us -> 22.9 us  [whole_of(): x = lax.all_gather(x, axis, axis=dim, tiled=True)]
    unnamed x21 -> x36, local copies, waits for them, and re-layouts: 23.5 us -> 33.3 us
    ppermute x4, starting transfers between devices: 25.3 us -> 16.1 us  [from_behind(): return lax.ppermute(block, axis, route)]
  transfers between devices with their start and end apart: 9 -> 9, of which waited for: 5 -> 6; matrix products, arithmetic and copies ran while one was open for 10% -> 12% of each run, Pallas kernels for 0% -> 0%
where the time goes in v1:
time: 586 us; the launch traced here: 585 us
  waiting for transfers between devices  340 us (58%)
  starting transfers between devices  84.3 us (14%)
  blocking collectives  47.1 us (8%)
  local copies, waits for them, and re-layouts  43.4 us (7%)
  between operations  27.8 us (5%)
  matrix products  25.2 us (4%)
  other arithmetic  17.2 us (3%)
    reduce_scatter x1, waiting for transfers between devices, per_device(): lax.psum_scatter(lax.dot_general(scaled, weights, (((1,), (1,)), ((), ())...  170 us
    ppermute x4, waiting for transfers between devices, from_behind(): return lax.ppermute(block, axis, route)  146 us
    all_to_all x1, starting transfers between devices, per_device(): lax.all_to_all(jnp.stack(jnp.split(target, lax.axis_size(DP), axis=1)), D...  63.8 us
    unnamed x2, blocking collectives  47.1 us
    unnamed x36, local copies, waits for them, and re-layouts  33.3 us
    all_gather x2, waiting for transfers between devices, whole_of(): x = lax.all_gather(x, axis, axis=dim, tiled=True)  22.9 us
    ppermute x4, starting transfers between devices, from_behind(): return lax.ppermute(block, axis, route)  16.1 us
  transfers between devices with their start and end apart: 9, of which 6 were waited for; matrix products, arithmetic and copies ran while one was open for 12% of the time, Pallas kernels for 0%

profile of v1, /device:TPU:1, one launch (start us, length us, event | category | flops | bytes accessed | tf_op | source)
XLA Modules:
  0.0 584.9 jit_solution(14665417726846585409)
XLA Ops:
  7.2 0.0 all-gather.5.cloned.1.call-start
  7.2 0.7 all-gather.5.cloned.1.call-update
  7.9 0.0 all-gather.7.cloned.1.call-start
  8.0 0.7 slice.3
  8.7 1.3 fusion.52
  10.0 0.8 convert_reduce_fusion
  10.9 1.5 fusion.42
  19.2 7.5 %constant_dynamic-slice_fusion = (bf16[1,128,7168]{2,1,0:T(8,128)(2,1)}, bf16[1,128,7168]{2,1,0:T(8,128)(2,1)}, bf16[1,128,7168]{2,1,0:T(8,128)(2,1)}, bf16[1,128,7168]{2,1,0:T(8,128)(2,1)}, bf16[1,128,7168]{2,1,0:T(8,128)(2,1)}) fusion(bf16[4,128,7168]{2,1,0:T(8,128)(2,1)} %param.7, s32[]{:T(128)S(6)} %min.20, s32[]{:T(128)S(6)} %min.19, s32[]{:T(128)S(6)} %min.18, ...), kind=kLoop, calls=%fused_computation.74 | loop fusion | bytes 18350100 | tf_op jit(solution)/shard_map/jit(dynamic_index_in_dim)/dynamic_slice | solution.py:57
  26.7 3.9 copy.30
  30.6 2.9 select_bitcast_fusion.3
  33.5 9.7 %collective-permute-start = (bf16[128,7168]{0,1:T(8,128)(2,1)}, bf16[128,7168]{0,1:T(8,128)(2,1)}, u32[]{:S(2)}, u32[]{:S(2)}) collective-permute-start(bf16[128,7168]{0,1:T(8,128)(2,1)} %select_bitcast_fusion.3), channel_id=1, source_target_pairs={{0,32},{16,48},{32,64},{48,80},{64,96},{80,112},{96,128},{112,144}... | collective-permute-start | bytes 5505032 | tf_op jit(solution)/shard_map/ppermute | solution.py:15
  43.8 3.9 copy.31
  47.7 1.4 select_bitcast_fusion.2
  49.1 2.4 collective-permute-start.1
  52.2 3.9 copy.32
  56.1 2.9 select_bitcast_fusion.1
  59.0 2.7 collective-permute-start.2
  62.4 3.9 copy.33
  66.3 22.8 %all-gather.5.cloned.1.call-done = bf16[1,512,2048]{2,1,0:T(8,128)(2,1)} async-done(((bf16[1,128,2048]{2,1,0:T(8,128)(2,1)}), bf16[1,512,2048]{2,1,0:T(8,128)(2,1)}) %all-gather.5.cloned.1.call-update) | async-done | bytes 2097168 | tf_op jit(solution)/shard_map/all_gather | solution.py:20
  89.1 0.0 all-gather.7.cloned.1.call-update
  89.1 1.4 select_bitcast_fusion
  90.5 1.3 collective-permute-start.3
  93.1 3.9 copy.34
  97.0 17.4 %collective-permute-done = bf16[128,7168]{0,1:T(8,128)(2,1)} collective-permute-done((bf16[128,7168]{0,1:T(8,128)(2,1)}, bf16[128,7168]{0,1:T(8,128)(2,1)}, u32[]{:S(2)}, u32[]{:S(2)}) %collective-permute-start) | collective-permute-done | bytes 1835040 | tf_op jit(solution)/shard_map/ppermute | solution.py:15
  114.3 27.4 %collective-permute-done.1 = bf16[128,7168]{0,1:T(8,128)(2,1)} collective-permute-done((bf16[128,7168]{0,1:T(8,128)(2,1)}, bf16[128,7168]{0,1:T(8,128)(2,1)}, u32[]{:S(2)}, u32[]{:S(2)}) %collective-permute-start.1) | collective-permute-done | bytes 1835040 | tf_op jit(solution)/shard_map/ppermute | solution.py:15
  141.7 63.2 %collective-permute-done.2 = bf16[128,7168]{0,1:T(8,128)(2,1)} collective-permute-done((bf16[128,7168]{0,1:T(8,128)(2,1)}, bf16[128,7168]{0,1:T(8,128)(2,1)}, u32[]{:S(2)}, u32[]{:S(2)}) %collective-permute-start.2) | collective-permute-done | bytes 1835040 | tf_op jit(solution)/shard_map/ppermute | solution.py:15
  204.9 38.3 %collective-permute-done.3 = bf16[128,7168]{0,1:T(8,128)(2,1)} collective-permute-done((bf16[128,7168]{0,1:T(8,128)(2,1)}, bf16[128,7168]{0,1:T(8,128)(2,1)}, u32[]{:S(2)}, u32[]{:S(2)}) %collective-permute-start.3) | collective-permute-done | bytes 1835040 | tf_op jit(solution)/shard_map/ppermute | solution.py:15
  243.2 3.3 fusion.4
  246.5 0.4 fusion.5
  246.8 0.7 fusion.35
  247.5 0.7 fusion.34
  248.2 0.7 fusion.33
  248.8 0.7 fusion.32
  249.5 0.7 fusion.31
  250.1 0.7 fusion.30
  250.8 0.7 fusion.29
  251.4 0.7 fusion.28
  252.1 0.7 fusion.27
  252.7 0.7 fusion.26
  253.4 0.7 fusion.25
  254.0 0.7 fusion.24
  254.7 0.7 fusion.23
  255.3 0.7 fusion.22
  256.0 0.7 fusion.21
  256.7 0.7 fusion.20
  257.3 63.8 %all-to-all-start = ((bf16[16,128,448]{1,2,0:T(8,128)(2,1)}), bf16[16,128,448]{1,2,0:T(8,128)(2,1)}, u32[]{:S(2)}, u32[]{:S(2)}) async-start(bf16[16,128,448]{1,2,0:T(8,128)(2,1)} %fusion.20), calls=%async_computation | async-start | bytes 3670016 | tf_op jit(solution)/shard_map/all_to_all | solution.py:72
  321.1 0.0 reduce-scatter.2.cloned.1.call-start
  321.8 0.6 dynamic-slice
  322.4 0.8 dynamic-update-slice
  323.2 39.9 %all-reduce = s32[4]{0:T(128)S(1)} all-reduce(s32[4]{0:T(128)S(1)} %dynamic-update-slice), channel_id=1, replica_groups=mesh['section'=16,'dp_0'=4,'dp_1'=4] {'dp_1'}, use_global_device_ids=true, to_apply=%add | all-reduce | flops 4 | bytes 32
  363.1 0.6 dynamic-slice.1
  364.3 0.2 dynamic-update-slice.1
  364.5 7.2 %all-reduce.1 = s32[16]{0:T(128)S(1)} all-reduce(s32[16]{0:T(128)S(1)} %dynamic-update-slice.1), channel_id=1, replica_groups=mesh['section'=16,'dp_0'=4,'dp_1'=4] {'dp_0'}, use_global_device_ids=true, to_apply=%add.1 | all-reduce | flops 16 | bytes 128
  371.7 0.6 reduce_sum.158
  373.1 0.1 select_reduce_fusion
  373.2 0.0 all-gather.7.cloned.1.call-done
  373.3 8.6 %fusion.6 = (f32[]{:T(128)}, f32[2048,448]{0,1:T(8,128)S(1)}) fusion(f32[2048]{0:T(1024)S(1)} %get-tuple-element.13, bf16[1,2048,448]{1,2,0:T(8,128)(2,1)S(1)} %copy-done, bf16[1,2048,2048]{2,1,0:T(8,128)(2,1)} %all-gather.7.cloned.1.call-done, bf16[16,128,448]{1,2,0:T(8,128)(2,1)} %all-to-all-done), kind=kOutput, calls=%fused_computation.10 | convolution fusion | flops 3762683904 | bytes 15736836 | tf_op jit(solution)/shard_map/dot_general | solution.py:83
  381.9 1.8 copy-done.4
  383.7 6.8 %convolution_convert_fusion = bf16[2048,2048]{1,0:T(8,128)(2,1)} fusion(bf16[1,2048,448]{1,2,0:T(8,128)(2,1)S(1)} %copy-done, f32[2048,448]{0,1:T(8,128)S(1)} %get-tuple-element.23, f32[2048]{0:T(1024)S(1)} %broadcast_select_fusion), kind=kOutput, calls=%fused_computation.4 | convolution fusion | flops 3764125696 | bytes 13901824 | tf_op jit(solution)/shard_map/dot_general | solution.py:90
  390.5 1.2 broadcast_in_dim.52
  391.8 4.3 all-to-all-start.1
  396.1 9.8 %fusion.12 = bf16[1,2048,448]{1,2,0:T(8,128)(2,1)} fusion(bf16[1,2048,2048]{2,1,0:T(8,128)(2,1)} %all-gather.7.cloned.1.call-done, f32[2048,448]{0,1:T(8,128)} %copy-done.4, f32[2048]{0:T(1024)S(1)} %broadcast_select_fusion), kind=kOutput, calls=%fused_computation.15 | convolution fusion | flops 3760848896 | bytes 13901824 | tf_op jit(solution)/shard_map/dot_general | solution.py:97
  405.9 0.6 reduce_sum.173
  407.2 170.1 %reduce-scatter.2.cloned.1.call-done = bf16[128,2048]{1,0:T(8,128)(2,1)} async-done(((bf16[2048,2048]{1,0:T(8,128)(2,1)}), bf16[128,2048]{1,0:T(8,128)(2,1)}) %reduce-scatter.2.cloned.1.call-update) | async-done | bytes 524304 | tf_op jit(solution)/shard_map/reduce_scatter | solution.py:89
  (18 shorter events, 0.1 us)
Async XLA Ops:
  7.2 366.1 %copy-start = (bf16[1,2048,448]{1,2,0:T(8,128)(2,1)S(1)}, bf16[1,2048,448]{1,2,0:T(8,128)(2,1)}, u32[]{:S(2)}) copy-start(bf16[1,2048,448]{1,2,0:T(8,128)(2,1)} %param.8) | copy-start | bytes 5505028
  7.2 81.9 %all-gather.5.cloned.1.call-start = ((), (), s32[]{:S(2)}) async-start(), calls=%async_computation.4 | async-start | bytes 2621440 | tf_op jit(solution)/shard_map/all_gather | solution.py:20
  7.9 365.3 %all-gather.7.cloned.1.call-start = ((), (), s32[]{:S(2)}) async-start(), calls=%async_computation.5 | async-start | bytes 10485760 | tf_op jit(solution)/shard_map/all_gather | solution.py:20
  33.5 80.8 %collective-permute-start = (bf16[128,7168]{0,1:T(8,128)(2,1)}, bf16[128,7168]{0,1:T(8,128)(2,1)}, u32[]{:S(2)}, u32[]{:S(2)}) collective-permute-start(bf16[128,7168]{0,1:T(8,128)(2,1)} %select_bitcast_fusion.3), channel_id=1, source_target_pairs={{0,32},{16,48},{32,64},{48,80},{64,96},{80,112},{96,128},{112,144}... | collective-permute-start | bytes 5505032 | tf_op jit(solution)/shard_map/ppermute | solution.py:15
  49.1 92.6 %collective-permute-start.1 = (bf16[128,7168]{0,1:T(8,128)(2,1)}, bf16[128,7168]{0,1:T(8,128)(2,1)}, u32[]{:S(2)}, u32[]{:S(2)}) collective-permute-start(bf16[128,7168]{0,1:T(8,128)(2,1)} %select_bitcast_fusion.2), channel_id=1, source_target_pairs={{0,16},{16,32},{32,48},{48,64},{64,80},{80,96},{96,112},{112,128},... | collective-permute-start | bytes 5505032 | tf_op jit(solution)/shard_map/ppermute | solution.py:15
  59.0 145.9 %collective-permute-start.2 = (bf16[128,7168]{0,1:T(8,128)(2,1)}, bf16[128,7168]{0,1:T(8,128)(2,1)}, u32[]{:S(2)}, u32[]{:S(2)}) collective-permute-start(bf16[128,7168]{0,1:T(8,128)(2,1)} %select_bitcast_fusion.1), channel_id=1, source_target_pairs={{16,0},{32,16},{48,32},{64,48},{80,64},{96,80},{112,96},{128,112},... | collective-permute-start | bytes 5505032 | tf_op jit(solution)/shard_map/ppermute | solution.py:15
  90.5 152.7 %collective-permute-start.3 = (bf16[128,7168]{0,1:T(8,128)(2,1)}, bf16[128,7168]{0,1:T(8,128)(2,1)}, u32[]{:S(2)}, u32[]{:S(2)}) collective-permute-start(bf16[128,7168]{0,1:T(8,128)(2,1)} %select_bitcast_fusion), channel_id=1, source_target_pairs={{32,0},{48,16},{64,32},{80,48},{96,64},{112,80},{128,96},{144,112}... | collective-permute-start | bytes 5505032 | tf_op jit(solution)/shard_map/ppermute | solution.py:15
  257.3 64.5 %copy-start.3 = (u32[256]{0:T(256)S(1)}, u32[256]{0:T(256)}, u32[]{:S(2)}) copy-start(u32[256]{0:T(256)} %constant.84) | copy-start | bytes 3076
  257.3 105.7 %copy-start.2 = (u32[256]{0:T(256)S(1)}, u32[256]{0:T(256)}, u32[]{:S(2)}) copy-start(u32[256]{0:T(256)} %constant.89) | copy-start | bytes 3076
  257.3 115.9 %all-to-all-start = ((bf16[16,128,448]{1,2,0:T(8,128)(2,1)}), bf16[16,128,448]{1,2,0:T(8,128)(2,1)}, u32[]{:S(2)}, u32[]{:S(2)}) async-start(bf16[16,128,448]{1,2,0:T(8,128)(2,1)} %fusion.20), calls=%async_computation | async-start | bytes 3670016 | tf_op jit(solution)/shard_map/all_to_all | solution.py:72
  321.1 256.2 %reduce-scatter.2.cloned.1.call-start = ((), (), s32[]{:S(2)}) async-start(), calls=%async_computation.3 | async-start | bytes 8912896 | tf_op jit(solution)/shard_map/reduce_scatter | solution.py:89
  381.9 1.8 copy-start.4
  391.8 14.1 %all-to-all-start.1 = ((f32[16,1,1]{2,1,0:T(1,128)}), f32[16,1,1]{2,1,0:T(1,128)S(1)}, u32[]{:S(2)}, u32[]{:S(2)}) async-start(f32[16,1,1]{2,1,0:T(1,128)} %broadcast_in_dim.52), calls=%async_computation.2 | async-start | bytes 16384 | tf_op jit(solution)/shard_map/all_to_all | solution.py:26
  396.1 181.2 %copy-start.1 = (bf16[1,2048,448]{1,2,0:T(8,128)(2,1)S(1)}, bf16[1,2048,448]{1,2,0:T(8,128)(2,1)}, u32[]{:S(2)}) copy-start(bf16[1,2048,448]{1,2,0:T(8,128)(2,1)} %param.8) | copy-start | bytes 5505028
Sparse Core Ops, SparseCore 0:
  9.8 79.2 all-gather.4
  90.9 225.9 all-gather.6
  390.6 186.6 reduce-scatter.1
